TPU v7x, 32 devices: a whole 2x2x4 slice. The times are simulated.
32 devices in a mesh: seq: 8 (over z, y), tp: 4 (over x, core).
Axes of the slice: x: 2, y: 2, z: 4, core: 2. Of those that a mesh axis runs over, the one named last changes fastest.
Arguments:
- inputs: bfloat16 [2, 32, 8192], P(None, 'seq', 'tp'), may hold values from -6 to 6
- out_grad: bfloat16 [2, 32, 8192], P(None, 'seq', 'tp'), may hold values from -6 to 6
- gate_weight: bfloat16 [8192, 14848], P('tp', 'seq'), may hold values from -0.0625 to 0.0625
- up_weight: bfloat16 [8192, 14848], P('tp', 'seq'), may hold values from -0.0625 to 0.0625
- down_weight: bfloat16 [14848, 8192], P('seq', 'tp'), may hold values from -0.0625 to 0.0625
Outputs:
- input_grad: bfloat16 [2, 32, 8192], P(None, 'seq', 'tp')
- gate_grad: float32 [8192, 14848], P('tp', 'seq')
- up_grad: float32 [8192, 14848], P('tp', 'seq')
- down_grad: float32 [14848, 8192], P('seq', 'tp')
All inputs are finite; a program needn't handle non-finite values.
Results may differ from a plain program's by a relative error of at most 0.0049.
Values may be sent and summed in bfloat16 or wider, within the bound.
A program may use at most 128 MiB of HBM per device.

v0:
```python
import jax
import jax.numpy as jnp
from jax import lax
from jax.sharding import PartitionSpec as P


def per_device(inputs, out_grad, gate_weight, up_weight, down_weight):
    blocks = inputs.shape[0]
    local_rows = inputs.shape[1]
    width_count = lax.axis_size("tp")
    block_tokens = local_rows * lax.axis_size("seq")
    share_rows = block_tokens // width_count
    share_start = lax.axis_index("tp") * share_rows
    contract_first = (((0,), (0,)), ((), ()))
    contract_last = (((1,), (1,)), ((), ()))
    totals = None
    results = [None] * blocks
    for index in range(blocks):
        whole_in = lax.all_gather(inputs[index], "seq", axis=0, tiled=True)
        whole_grad = lax.all_gather(out_grad[index], "seq", axis=0, tiled=True)
        gate_part = jnp.dot(whole_in, gate_weight, preferred_element_type=jnp.float32)
        up_part = jnp.dot(whole_in, up_weight, preferred_element_type=jnp.float32)
        gate, up_proj = lax.psum((gate_part, up_part), "tp")
        hidden_share = lax.psum_scatter(
            lax.dot_general(
                whole_grad, down_weight, contract_last, preferred_element_type=jnp.float32
            ),
            "tp",
            scatter_dimension=0,
            tiled=True,
        )
        gate_share = lax.dynamic_slice_in_dim(gate, share_start, share_rows, 0)
        up_share = lax.dynamic_slice_in_dim(up_proj, share_start, share_rows, 0)
        sig = jax.nn.sigmoid(gate_share)
        up_local = (hidden_share * gate_share * sig).astype(jnp.bfloat16)
        gate_local = (hidden_share * up_share * sig * (1.0 + gate_share * (1.0 - sig))).astype(
            jnp.bfloat16
        )
        front_unit_gate = lax.all_gather(gate_local, "tp", axis=0, tiled=True)
        front_unit_up = lax.all_gather(up_local, "tp", axis=0, tiled=True)
        hidden = (jax.nn.silu(gate) * up_proj).astype(jnp.bfloat16)
        down_term = lax.dot_general(
            hidden, whole_grad, contract_first, preferred_element_type=jnp.float32
        )
        gate_term = lax.dot_general(
            whole_in, front_unit_gate, contract_first, preferred_element_type=jnp.float32
        )
        up_term = lax.dot_general(
            whole_in, front_unit_up, contract_first, preferred_element_type=jnp.float32
        )
        terms = (gate_term, up_term, down_term)
        if totals is None:
            totals = terms
        else:
            totals = (totals[0] + terms[0], totals[1] + terms[1], totals[2] + terms[2])
        first = lax.dot_general(
            front_unit_gate, gate_weight, contract_last, preferred_element_type=jnp.float32
        )
        second = lax.dot_general(
            front_unit_up, up_weight, contract_last, preferred_element_type=jnp.float32
        )
        results[index] = lax.psum_scatter(
            first + second, "seq", scatter_dimension=0, tiled=True
        ).astype(jnp.bfloat16)
    return (jnp.stack(results), totals[0], totals[1], totals[2])


def solution(mesh):
    return jax.shard_map(
        per_device,
        mesh=mesh,
        in_specs=(
            P(None, "seq", "tp"),
            P(None, "seq", "tp"),
            P("tp", "seq"),
            P("tp", "seq"),
            P("seq", "tp"),
        ),
        out_specs=(P(None, "seq", "tp"), P("tp", "seq"), P("tp", "seq"), P("seq", "tp")),
        check_vma=False,
    )
```

profile of v0, /device:TPU:0, one launch (start us, length us, event | category | flops | bytes accessed | tf_op | source)
XLA Modules:
  0.0 335.3 jit_solution(6774601214005411477)
XLA Ops:
  7.2 0.9 fusion.32
  8.2 32.8 %all-gather.3 = bf16[1,32,2048]{2,0,1:T(2,128)(2,1)S(1)} all-gather(bf16[1,4,2048]{2,0,1:T(2,128)(2,1)S(1)} %copy.24), channel_id=5, replica_groups=mesh['seq'=8,'tp'=4] {'seq'}, dimensions={1}, use_global_device_ids=true | all-gather | bytes 147456 | tf_op jit(solution)/shard_map/all_gather | solution.py:19
  41.1 30.7 %all-gather.1 = bf16[1,32,2048]{2,0,1:T(2,128)(2,1)S(1)} all-gather(bf16[1,4,2048]{2,0,1:T(2,128)(2,1)S(1)} %copy.22), channel_id=3, replica_groups=mesh['seq'=8,'tp'=4] {'seq'}, dimensions={1}, use_global_device_ids=true | all-gather | bytes 147456 | tf_op jit(solution)/shard_map/all_gather | solution.py:19
  71.9 6.4 %fusion.13 = f32[32,1856]{1,0:T(8,128)} fusion(bf16[2048,1856]{0,1:T(8,128)(2,1)} %param.7, bf16[1,32,2048]{2,1,0:T(8,128)(2,1)S(1)} %copy.18), kind=kOutput, calls=%fused_computation.20 | convolution fusion | flops 243269632 | bytes 7970816 | tf_op jit(solution)/shard_map/dot_general | solution.py:21
  78.3 3.0 fusion.15
  81.4 3.0 fusion.2
  84.4 3.0 fusion.4
  87.5 30.7 %all-gather.2 = bf16[1,32,2048]{2,0,1:T(2,128)(2,1)S(1)} all-gather(bf16[1,4,2048]{2,0,1:T(2,128)(2,1)S(1)} %copy.23), channel_id=4, replica_groups=mesh['seq'=8,'tp'=4] {'seq'}, dimensions={1}, use_global_device_ids=true | all-gather | bytes 147456 | tf_op jit(solution)/shard_map/all_gather | solution.py:20
  118.3 32.9 %all-gather = bf16[1,32,2048]{2,0,1:T(2,128)(2,1)} all-gather(bf16[1,4,2048]{2,0,1:T(2,128)(2,1)S(1)} %copy.21), channel_id=2, replica_groups=mesh['seq'=8,'tp'=4] {'seq'}, dimensions={1}, use_global_device_ids=true | all-gather | bytes 147456 | tf_op jit(solution)/shard_map/all_gather | solution.py:20
  151.2 4.0 %fusion.19 = f32[32,1856]{1,0:T(8,128)} fusion(bf16[1856,2048]{1,0:T(8,128)(2,1)S(1)} %bitcast.63, bf16[1,32,2048]{2,0,1:T(2,128)(2,1)} %all-gather), kind=kOutput, calls=%fused_computation.26 | convolution fusion | flops 243269632 | bytes 7970816 | tf_op jit(solution)/shard_map/dot_general | solution.py:25
  155.2 3.0 fusion.7
  158.3 0.6 dynamic-slice.2
  159.0 0.6 dynamic-slice
  160.8 40.2 %all-reduce.9.cloned.1.call-done = (f32[32,1856]{1,0:T(8,128)}, f32[32,1856]{1,0:T(8,128)}, f32[32,1856]{1,0:T(8,128)}, f32[32,1856]{1,0:T(8,128)}, f32[32,1856]{1,0:T(8,128)}, /*index=5*/f32[32,1856]{1,0:T(8,128)}) async-done(((f32[32,1856]{1,0:T(8,128)}, f32[32,1856]{1,0:T(8,128)}, f32[32,1856]{1,0:T(8,128)}, f32[32,1856]{1,0:T(8,128)}, f32[32,1856]{1,0:T(8,128)}, /*index=5*/f32[32,1856]{1,0:T(8,128)}), ...) | async-done | bytes 1425424 | tf_op jit(solution)/shard_map/psum | solution.py:23
  201.0 3.5 %fusion.17 = f32[1856,2048]{1,0:T(8,128)S(1)} fusion(f32[32,1856]{1,0:T(8,128)} %get-tuple-element.9, f32[32,1856]{1,0:T(8,128)} %get-tuple-element.11, bf16[1,32,2048]{2,0,1:T(2,128)(2,1)} %all-gather), kind=kOutput, calls=%fused_computation.24 | convolution fusion | flops 243625984 | bytes 15810560 | tf_op jit(solution)/shard_map/dot_general | solution.py:42
  204.5 0.9 multiply_convert_fusion.6
  205.5 5.4 %all_gather.26 = bf16[32,1856]{1,0:T(8,128)(2,1)S(1)} all-gather(bf16[8,1856]{1,0:T(8,128)(2,1)S(1)} %get-tuple-element.13), channel_id=1, replica_groups=mesh['seq'=8,'tp'=4] {'tp'}, dimensions={0}, use_global_device_ids=true | all-gather | bytes 148480 | tf_op jit(solution)/shard_map/all_gather | solution.py:39
  210.9 1.4 fusion.33
  212.3 7.8 %fusion.11 = f32[1856,2048]{1,0:T(8,128)} fusion(bf16[32,1856]{1,0:T(8,128)(2,1)S(1)} %all_gather.26, bf16[1,32,2048]{2,1,0:T(8,128)(2,1)S(1)} %copy-done.2), kind=kOutput, calls=%fused_computation.18 | convolution fusion | flops 243269632 | bytes 15454208 | tf_op jit(solution)/shard_map/dot_general | solution.py:45
  220.1 0.9 multiply_convert_fusion.4
  221.0 5.5 %all_gather.31 = bf16[32,1856]{1,0:T(8,128)(2,1)S(1)} all-gather(bf16[8,1856]{1,0:T(8,128)(2,1)S(1)} %get-tuple-element.14), channel_id=1, replica_groups=mesh['seq'=8,'tp'=4] {'tp'}, dimensions={0}, use_global_device_ids=true | all-gather | bytes 148480 | tf_op jit(solution)/shard_map/all_gather | solution.py:40
  226.5 5.4 %all_gather.27 = bf16[32,1856]{1,0:T(8,128)(2,1)S(1)} all-gather(bf16[8,1856]{1,0:T(8,128)(2,1)S(1)} %get-tuple-element.12), channel_id=1, replica_groups=mesh['seq'=8,'tp'=4] {'tp'}, dimensions={0}, use_global_device_ids=true | all-gather | bytes 148480 | tf_op jit(solution)/shard_map/all_gather | solution.py:40
  231.9 5.6 %all_gather.30 = bf16[32,1856]{1,0:T(8,128)(2,1)S(1)} all-gather(bf16[8,1856]{1,0:T(8,128)(2,1)S(1)} %get-tuple-element.15), channel_id=1, replica_groups=mesh['seq'=8,'tp'=4] {'tp'}, dimensions={0}, use_global_device_ids=true | all-gather | bytes 148480 | tf_op jit(solution)/shard_map/all_gather | solution.py:39
  237.5 7.8 %fusion.9 = f32[1856,2048]{1,0:T(8,128)} fusion(bf16[32,1856]{1,0:T(8,128)(2,1)S(1)} %all_gather.27, bf16[1,32,2048]{2,1,0:T(8,128)(2,1)S(1)} %copy-done.2), kind=kOutput, calls=%fused_computation.16 | convolution fusion | flops 243269632 | bytes 15454208 | tf_op jit(solution)/shard_map/dot_general | solution.py:48
  245.3 2.1 convolution_add_fusion.2
  247.5 1.4 fusion.34
  248.9 1.4 convolution_add_fusion.1
  250.3 7.8 %convolution_add_fusion = f32[1856,2048]{1,0:T(8,128)} fusion(f32[1856,2048]{1,0:T(8,128)S(1)} %fusion.17, f32[32,1856]{1,0:T(8,128)S(1)} %copy-done.6, f32[32,1856]{1,0:T(8,128)S(1)} %copy-done.7, bf16[1,32,2048]{2,0,1:T(2,128)(2,1)S(1)} %copy-done.4), kind=kOutput, calls=%fused_computation.2 | convolution fusion | flops 247427072 | bytes 31014912 | tf_op jit(solution)/shard_map/dot_general | solution.py:42
  258.2 13.1 %add_bitcast_fusion = f32[2048,1856]{0,1:T(8,128)} fusion(f32[1856,2048]{1,0:T(8,128)} %fusion.9, bf16[32,1856]{1,0:T(8,128)(2,1)S(1)} %all_gather.31, bf16[1,32,2048]{2,1,0:T(8,128)(2,1)S(1)} %copy.20), kind=kOutput, calls=%fused_computation | convolution fusion | flops 247070720 | bytes 30658560 | tf_op jit(solution)/shard_map/dot_general | solution.py:48
  271.3 13.2 %add_bitcast_fusion.1 = f32[2048,1856]{0,1:T(8,128)} fusion(f32[1856,2048]{1,0:T(8,128)} %fusion.11, bf16[32,1856]{1,0:T(8,128)(2,1)S(1)} %all_gather.30, bf16[1,32,2048]{2,1,0:T(8,128)(2,1)S(1)} %copy.20), kind=kOutput, calls=%fused_computation.1 | convolution fusion | flops 247070720 | bytes 30658560 | tf_op jit(solution)/shard_map/dot_general | solution.py:45
  284.5 43.3 %all-reduce.10 = (bf16[32,2048]{1,0:T(8,128)(2,1)S(1)}, bf16[32,2048]{1,0:T(8,128)(2,1)S(1)}) all-reduce(f32[32,2048]{1,0:T(8,128)S(1)} %convolution_add_fusion.1, f32[32,2048]{1,0:T(8,128)S(1)} %copy-done.5), channel_id=9, replica_groups=mesh['seq'=8,'tp'=4] {'seq'}, use_global_device_ids=true, to_apply=%region_7.8.clone | all-reduce | flops 131072 | bytes 786432
  327.8 0.6 pad_maximum_fusion
  (52 shorter events, 0.5 us)
Async XLA Ops:
  7.2 193.8 %all-reduce.9.cloned.1.call-start = ((), (), s32[]{:S(2)}) async-start(), calls=%async_computation | async-start | bytes 2949120 | tf_op jit(solution)/shard_map/psum | solution.py:23
  7.2 71.1 %copy-start = (bf16[2048,1856]{0,1:T(8,128)(2,1)S(1)}, bf16[2048,1856]{0,1:T(8,128)(2,1)}, u32[]{:S(2)}) copy-start(bf16[2048,1856]{0,1:T(8,128)(2,1)} %param.8) | copy-start | bytes 22806532
  71.9 6.4 %copy-start.1 = (bf16[1,32,2048]{2,1,0:T(8,128)(2,1)}, bf16[1,32,2048]{2,1,0:T(8,128)(2,1)S(1)}, u32[]{:S(2)}) copy-start(bf16[1,32,2048]{2,1,0:T(8,128)(2,1)S(1)} %copy.18) | copy-start | bytes 393220
  71.9 9.4 %slice-start = ((s8[7602176]{0:T(1024)(128)(4,1)}), s8[4194304]{0:T(1024)(128)(4,1)S(1)}, s32[]{:S(2)}) async-start(s8[7602176]{0:T(1024)(128)(4,1)} %bitcast.56), calls=%async_computation.1 | async-start | bytes 8388608
  78.3 3.0 slice-start.1
  81.3 6.1 %copy-start.8 = (bf16[2,4,2048]{2,1,0:T(4,128)(2,1)S(1)}, bf16[2,4,2048]{2,1,0:T(4,128)(2,1)}, u32[]{:S(2)}) copy-start(bf16[2,4,2048]{2,1,0:T(4,128)(2,1)} %param.6) | copy-start | bytes 98308
  81.3 69.8 %slice-start.6 = ((s8[7602176]{0:T(1024)(128)(4,1)}), s8[4194304]{0:T(1024)(128)(4,1)S(1)}, s32[]{:S(2)}) async-start(s8[7602176]{0:T(1024)(128)(4,1)} %bitcast.62), calls=%async_computation.7 | async-start | bytes 8388608
  84.4 66.8 %slice-start.7 = ((s8[7602176]{0:T(1024)(128)(4,1)}), s8[3407872]{0:T(1024)(128)(4,1)S(1)}, s32[]{:S(2)}) async-start(s8[7602176]{0:T(1024)(128)(4,1)} %bitcast.62), calls=%async_computation.8 | async-start | bytes 6815744
  118.3 37.0 %copy-start.3 = (bf16[1,32,2048]{2,0,1:T(2,128)(2,1)}, bf16[1,32,2048]{2,0,1:T(2,128)(2,1)S(1)}, u32[]{:S(2)}) copy-start(bf16[1,32,2048]{2,0,1:T(2,128)(2,1)S(1)} %all-gather.2) | copy-start | bytes 393220
  151.2 7.1 %copy-start.10 = (u32[32]{0:T(128)S(1)}, u32[32]{0:T(128)}, u32[]{:S(2)}) copy-start(u32[32]{0:T(128)} %constant.23) | copy-start | bytes 388
  151.2 7.8 %copy-start.9 = (u32[32]{0:T(128)S(1)}, u32[32]{0:T(128)}, u32[]{:S(2)}) copy-start(u32[32]{0:T(128)} %constant.19) | copy-start | bytes 388
  158.3 52.6 %slice-start.2 = ((s8[7602176]{0:T(1024)(128)(4,1)}), s8[3407872]{0:T(1024)(128)(4,1)S(1)}, s32[]{:S(2)}) async-start(s8[7602176]{0:T(1024)(128)(4,1)} %bitcast.58), calls=%async_computation.3 | async-start | bytes 6815744
  201.0 9.9 %slice-start.3 = ((s8[7602176]{0:T(1024)(128)(4,1)}), s8[4194304]{0:T(1024)(128)(4,1)S(1)}, s32[]{:S(2)}) async-start(s8[7602176]{0:T(1024)(128)(4,1)} %bitcast.58), calls=%async_computation.4 | async-start | bytes 8388608
  210.9 1.4 copy-start.2
  212.3 7.8 %copy-start.6 = (f32[32,1856]{1,0:T(8,128)S(1)}, f32[32,1856]{1,0:T(8,128)}, u32[]{:S(2)}) copy-start(f32[32,1856]{1,0:T(8,128)} %get-tuple-element.6) | copy-start | bytes 712708
  212.3 7.8 %copy-start.7 = (f32[32,1856]{1,0:T(8,128)S(1)}, f32[32,1856]{1,0:T(8,128)}, u32[]{:S(2)}) copy-start(f32[32,1856]{1,0:T(8,128)} %get-tuple-element.8) | copy-start | bytes 712708
  212.3 33.0 %slice-start.4 = ((s8[7602176]{0:T(1024)(128)(4,1)}), s8[4194304]{0:T(1024)(128)(4,1)S(1)}, s32[]{:S(2)}) async-start(s8[7602176]{0:T(1024)(128)(4,1)} %bitcast.60), calls=%async_computation.5 | async-start | bytes 8388608
  221.0 24.3 %slice-start.5 = ((s8[7602176]{0:T(1024)(128)(4,1)}), s8[3407872]{0:T(1024)(128)(4,1)S(1)}, s32[]{:S(2)}) async-start(s8[7602176]{0:T(1024)(128)(4,1)} %bitcast.60), calls=%async_computation.6 | async-start | bytes 6815744
  248.9 1.5 copy-start.4
  271.3 13.2 %copy-start.5 = (f32[32,2048]{1,0:T(8,128)S(1)}, f32[32,2048]{1,0:T(8,128)}, u32[]{:S(2)}) copy-start(f32[32,2048]{1,0:T(8,128)} %convolution_add_fusion.2) | copy-start | bytes 786436
Sparse Core Ops, SparseCore 0:
  158.4 42.5 all-reduce.8
where the time goes:
time: 336 us; the launch traced here: 335 us
  blocking collectives  192 us (57%)
  matrix products  82.2 us (24%)
  waiting for transfers between devices  40.2 us (12%)
  between operations  15.5 us (5%)
    all_gather x2, blocking collectives, per_device(): whole_grad = lax.all_gather(out_grad[index], 'seq', axis=0, tiled=True)  63.7 us
    all_gather x2, blocking collectives, per_device(): whole_in = lax.all_gather(inputs[index], 'seq', axis=0, tiled=True)  63.6 us
    unnamed x1, blocking collectives  43.3 us
    psum x1, waiting for transfers between devices, per_device(): gate, up_proj = lax.psum((gate_part, up_part), 'tp')  40.2 us
    dot_general x2, matrix products, per_device(): lax.dot_general(whole_in, front_unit_gate, contract_first, preferred_elem...  21 us
    dot_general x2, matrix products, per_device(): lax.dot_general(whole_in, front_unit_up, contract_first, preferred_elemen...  20.9 us
    dot_general x2, matrix products, per_device(): lax.dot_general(hidden, whole_grad, contract_first, preferred_element_typ...  11.4 us
    all_gather x2, blocking collectives, per_device(): front_unit_gate = lax.all_gather(gate_local, 'tp', axis=0, tiled=True)  11 us
  transfers between devices with their start and end apart: 1, of which 1 were waited for; matrix products, arithmetic and copies ran while one was open for 0% of the time, Pallas kernels for 0%

commit v1 on v0

--- a/solution.py
+++ b/solution.py
@@ -2,6 +2,17 @@
 import jax.numpy as jnp
 from jax import lax
 from jax.sharding import PartitionSpec as P
+
+
+def gather_by_hops(value, axis, d):
+    size = lax.axis_size(axis)
+    route = [(i, (i + 1) % size) for i in range(size)]
+    shards = [value]
+    for far in range(1, size):
+        shards = [lax.ppermute(shards[0], axis, route), *shards]
+    whole = jnp.concatenate(shards, axis=d)
+    places = (lax.axis_index(axis) + 1) * shards[-1].shape[d]
+    return jnp.roll(whole, places, axis=d)
 
 
 def per_device(inputs, out_grad, gate_weight, up_weight, down_weight):
@@ -17,7 +28,7 @@
     results = [None] * blocks
     for index in range(blocks):
         whole_in = lax.all_gather(inputs[index], "seq", axis=0, tiled=True)
-        whole_grad = lax.all_gather(out_grad[index], "seq", axis=0, tiled=True)
+        whole_grad = gather_by_hops(out_grad[index], "seq", 0)
         gate_part = jnp.dot(whole_in, gate_weight, preferred_element_type=jnp.float32)
         up_part = jnp.dot(whole_in, up_weight, preferred_element_type=jnp.float32)
         gate, up_proj = lax.psum((gate_part, up_part), "tp")

time: 336 us -> 301 us (0.90)
  blocking collectives: 192 us -> 128 us
  waiting for transfers between devices: 40.2 us -> 53.8 us
  starting transfers between devices: 0.04 us -> 8.88 us
  matrix products: 82.2 us -> 88.4 us
    all_gather x2 -> x0, blocking collectives: 63.7 us -> none  [per_device(): whole_grad = lax.all_gather(out_grad[index], 'seq', axis=0, tiled=True)]
    ppermute x0 -> x14, waiting for transfers between devices: none -> 13.7 us  [gather_by_hops(): shards = [lax.ppermute(shards[0], axis, route), *shards]]
    ppermute x0 -> x14, starting transfers between devices: none -> 8.84 us  [gather_by_hops(): shards = [lax.ppermute(shards[0], axis, route), *shards]]
    dot_general x2, matrix products: 7.05 us -> 12.4 us  [per_device(): lax.dot_general(whole_grad, down_weight, contract_last, preferred_element...]
  transfers between devices with their start and end apart: 1 -> 15, of which waited for: 1 -> 7; matrix products, arithmetic and copies ran while one was open for 0% -> 8% of each run, Pallas kernels for 0% -> 0%
where the time goes in v1:
time: 301 us
  blocking collectives  128 us (43%)
  matrix products  88.4 us (29%)
  waiting for transfers between devices  53.8 us (18%)
  between operations  15.4 us (5%)
  starting transfers between devices  8.88 us (3%)
  local copies, waits for them, and re-layouts  3.36 us (1%)
    all_gather x2, blocking collectives, per_device(): whole_in = lax.all_gather(inputs[index], 'seq', axis=0, tiled=True)  63 us
    unnamed x1, blocking collectives  43.3 us
    psum x1, waiting for transfers between devices, per_device(): gate, up_proj = lax.psum((gate_part, up_part), 'tp')  40.1 us
    dot_general x2, matrix products, per_device(): lax.dot_general(whole_in, front_unit_gate, contract_first, preferred_elem...  20.9 us
    dot_general x2, matrix products, per_device(): lax.dot_general(whole_in, front_unit_up, contract_first, preferred_elemen...  20.9 us
    ppermute x14, waiting for transfers between devices, gather_by_hops(): shards = [lax.ppermute(shards[0], axis, route), *shards]  13.7 us
    dot_general x2, matrix products, per_device(): lax.dot_general(whole_grad, down_weight, contract_last, preferred_element...  12.4 us
    all_gather x2, blocking collectives, per_device(): front_unit_gate = lax.all_gather(gate_local, 'tp', axis=0, tiled=True)  11 us
  transfers between devices with their start and end apart: 15, of which 7 were waited for; matrix products, arithmetic and copies ran while one was open for 8% of the time, Pallas kernels for 0%

profile of v1, /device:TPU:0, one launch (start us, length us, event | category | flops | bytes accessed | tf_op | source)
XLA Modules:
  0.0 300.5 jit_solution(7183698968443532285)
XLA Ops:
  8.1 3.0 %collective-permute-start = (bf16[4,2048]{1,0:T(4,128)(2,1)S(1)}, bf16[4,2048]{1,0:T(4,128)(2,1)S(1)}, u32[]{:S(2)}, u32[]{:S(2)}) collective-permute-start(bf16[4,2048]{1,0:T(4,128)(2,1)S(1)} %get-tuple-element.17), channel_id=1, source_target_pairs={{0,4},{4,8},{8,12},{12,16},{16,20},{20,24},{24,28},{28,0},{1,5},{5... | collective-permute-start | bytes 49160 | tf_op jit(solution)/shard_map/ppermute | solution.py:12
  11.2 1.5 collective-permute-start.7
  13.5 4.1 %collective-permute-done.7 = bf16[4,2048]{1,0:T(4,128)(2,1)S(1)} collective-permute-done((bf16[4,2048]{1,0:T(4,128)(2,1)S(1)}, bf16[4,2048]{1,0:T(4,128)(2,1)S(1)}, u32[]{:S(2)}, u32[]{:S(2)}) %collective-permute-start.7) | collective-permute-done | bytes 16416 | tf_op jit(solution)/shard_map/ppermute | solution.py:12
  17.6 30.9 %all-gather = bf16[1,32,2048]{2,0,1:T(2,128)(2,1)S(1)} all-gather(bf16[1,4,2048]{2,0,1:T(2,128)(2,1)S(1)} %copy.15), channel_id=2, replica_groups=mesh['seq'=8,'tp'=4] {'seq'}, dimensions={1}, use_global_device_ids=true | all-gather | bytes 147456 | tf_op jit(solution)/shard_map/all_gather | solution.py:30
  48.7 2.0 collective-permute-start.1
  50.8 6.2 %fusion.12 = f32[32,1856]{1,0:T(8,128)} fusion(bf16[2048,1856]{0,1:T(8,128)(2,1)} %param.9, bf16[1,32,2048]{2,1,0:T(8,128)(2,1)S(1)} %copy.13), kind=kOutput, calls=%fused_computation.23 | convolution fusion | flops 243269632 | bytes 7970816 | tf_op jit(solution)/shard_map/dot_general | solution.py:32
  57.5 3.1 %fusion.14 = f32[32,1856]{1,0:T(8,128)} fusion(bf16[2048,1856]{0,1:T(8,128)(2,1)S(1)} %copy-done, bf16[1,32,2048]{2,1,0:T(8,128)(2,1)S(1)} %copy.13), kind=kOutput, calls=%fused_computation.25 | convolution fusion | flops 243269632 | bytes 7970816 | tf_op jit(solution)/shard_map/dot_general | solution.py:33
  60.6 2.8 collective-permute-done.2
  64.2 32.0 %all-gather.1 = bf16[1,32,2048]{2,0,1:T(2,128)(2,1)S(1)} all-gather(bf16[1,4,2048]{2,0,1:T(2,128)(2,1)S(1)} %copy.16), channel_id=3, replica_groups=mesh['seq'=8,'tp'=4] {'seq'}, dimensions={1}, use_global_device_ids=true | all-gather | bytes 147456 | tf_op jit(solution)/shard_map/all_gather | solution.py:30
  97.2 3.0 %fusion.4 = f32[32,1856]{1,0:T(8,128)} fusion(bf16[2048,1856]{0,1:T(8,128)(2,1)S(1)} %bitcast.51, bf16[1,32,2048]{2,1,0:T(8,128)(2,1)S(1)} %copy.14), kind=kOutput, calls=%fused_computation.15 | convolution fusion | flops 243269632 | bytes 7970816 | tf_op jit(solution)/shard_map/dot_general | solution.py:32
  100.2 2.6 collective-permute-done.4
  103.5 3.0 %fusion.6 = f32[32,1856]{1,0:T(8,128)} fusion(bf16[2048,1856]{0,1:T(8,128)(2,1)S(1)} %copy-done, bf16[1,32,2048]{2,1,0:T(8,128)(2,1)S(1)} %copy.14), kind=kOutput, calls=%fused_computation.17 | convolution fusion | flops 243269632 | bytes 7970816 | tf_op jit(solution)/shard_map/dot_general | solution.py:33
  106.6 2.7 collective-permute-done.5
  110.1 6.2 %fusion.26 = f32[32,1856]{1,0:T(8,128)} fusion(bf16[1856,2048]{1,0:T(8,128)(2,1)} %param.11, s32[]{:T(128)S(6)} %select_n.20, bf16[32,2048]{1,0:T(8,128)(2,1)S(1)} %concatenate.10), kind=kOutput, calls=%fused_computation.46 | convolution fusion | flops 243531776 | bytes 7970820 | tf_op jit(solution)/shard_map/dot_general | solution.py:36
  116.5 6.2 %fusion.23 = f32[32,1856]{1,0:T(8,128)} fusion(bf16[1856,2048]{1,0:T(8,128)(2,1)} %param.11, s32[]{:T(128)S(6)} %select_n.20, bf16[32,2048]{1,0:T(8,128)(2,1)S(1)} %concatenate.9), kind=kOutput, calls=%fused_computation.45 | convolution fusion | flops 243531776 | bytes 7970820 | tf_op jit(solution)/shard_map/dot_general | solution.py:36
  125.1 40.1 %all-reduce.9.cloned.1.call-done = (f32[32,1856]{1,0:T(8,128)}, f32[32,1856]{1,0:T(8,128)}, f32[32,1856]{1,0:T(8,128)}, f32[32,1856]{1,0:T(8,128)}, f32[32,1856]{1,0:T(8,128)}, /*index=5*/f32[32,1856]{1,0:T(8,128)}) async-done(((f32[32,1856]{1,0:T(8,128)}, f32[32,1856]{1,0:T(8,128)}, f32[32,1856]{1,0:T(8,128)}, f32[32,1856]{1,0:T(8,128)}, f32[32,1856]{1,0:T(8,128)}, /*index=5*/f32[32,1856]{1,0:T(8,128)}), ...) | async-done | bytes 1425424 | tf_op jit(solution)/shard_map/psum | solution.py:34
  166.1 5.6 %all_gather.19 = bf16[32,1856]{1,0:T(8,128)(2,1)S(1)} all-gather(bf16[8,1856]{1,0:T(8,128)(2,1)S(1)} %get-tuple-element.14), channel_id=1, replica_groups=mesh['seq'=8,'tp'=4] {'tp'}, dimensions={0}, use_global_device_ids=true | all-gather | bytes 148480 | tf_op jit(solution)/shard_map/all_gather | solution.py:50
  171.6 4.6 %fusion.30 = f32[32,2048]{1,0:T(8,128)S(1)} fusion(bf16[32,1856]{1,0:T(8,128)(2,1)S(1)} %all_gather.19, bf16[2048,1856]{0,1:T(8,128)(2,1)} %param.9), kind=kOutput, calls=%fused_computation.48 | convolution fusion | flops 243269632 | bytes 7983104 | tf_op jit(solution)/shard_map/dot_general | solution.py:67
  176.2 7.8 %fusion.10 = f32[1856,2048]{1,0:T(8,128)} fusion(bf16[32,1856]{1,0:T(8,128)(2,1)S(1)} %all_gather.19, bf16[1,32,2048]{2,1,0:T(8,128)(2,1)S(1)} %copy.13), kind=kOutput, calls=%fused_computation.21 | convolution fusion | flops 243269632 | bytes 15454208 | tf_op jit(solution)/shard_map/dot_general | solution.py:56
  184.1 2.2 fusion.16
  186.3 1.0 multiply_convert_fusion.4
  187.3 5.4 %all_gather.23 = bf16[32,1856]{1,0:T(8,128)(2,1)S(1)} all-gather(bf16[8,1856]{1,0:T(8,128)(2,1)S(1)} %get-tuple-element.15), channel_id=1, replica_groups=mesh['seq'=8,'tp'=4] {'tp'}, dimensions={0}, use_global_device_ids=true | all-gather | bytes 148480 | tf_op jit(solution)/shard_map/all_gather | solution.py:51
  192.7 5.4 %all_gather.20 = bf16[32,1856]{1,0:T(8,128)(2,1)S(1)} all-gather(bf16[8,1856]{1,0:T(8,128)(2,1)S(1)} %get-tuple-element.13), channel_id=1, replica_groups=mesh['seq'=8,'tp'=4] {'tp'}, dimensions={0}, use_global_device_ids=true | all-gather | bytes 148480 | tf_op jit(solution)/shard_map/all_gather | solution.py:51
  198.1 5.4 %all_gather.22 = bf16[32,1856]{1,0:T(8,128)(2,1)S(1)} all-gather(bf16[8,1856]{1,0:T(8,128)(2,1)S(1)} %get-tuple-element.16), channel_id=1, replica_groups=mesh['seq'=8,'tp'=4] {'tp'}, dimensions={0}, use_global_device_ids=true | all-gather | bytes 148480 | tf_op jit(solution)/shard_map/all_gather | solution.py:50
  203.4 7.8 %fusion.8 = f32[1856,2048]{1,0:T(8,128)} fusion(bf16[32,1856]{1,0:T(8,128)(2,1)S(1)} %all_gather.20, bf16[1,32,2048]{2,1,0:T(8,128)(2,1)S(1)} %copy.13), kind=kOutput, calls=%fused_computation.19 | convolution fusion | flops 243269632 | bytes 15454208 | tf_op jit(solution)/shard_map/dot_general | solution.py:59
  211.3 1.4 convolution_add_fusion.2
  212.7 1.4 fusion.31
  214.1 1.4 convolution_add_fusion.1
  215.6 7.8 %convolution_add_fusion = f32[1856,2048]{1,0:T(8,128)} fusion(f32[1856,2048]{1,0:T(8,128)S(1)} %fusion.16, f32[32,1856]{1,0:T(8,128)S(1)} %copy-done.1, f32[32,1856]{1,0:T(8,128)S(1)} %copy-done.2, s32[]{:T(128)S(6)} %select_n.20, bf16[32,2048]{1,0:T(8,128)(2,1)S(1)} %concatenate.9), kind=kOutput, calls=%fused_computation.2 | convolution fusion | flops 247689216 | bytes 31014916 | tf_op jit(solution)/shard_map/dot_general | solution.py:53
  223.4 13.1 %add_bitcast_fusion = f32[2048,1856]{0,1:T(8,128)} fusion(f32[1856,2048]{1,0:T(8,128)} %fusion.8, bf16[32,1856]{1,0:T(8,128)(2,1)S(1)} %all_gather.23, bf16[1,32,2048]{2,1,0:T(8,128)(2,1)S(1)} %copy.14), kind=kOutput, calls=%fused_computation | convolution fusion | flops 247070720 | bytes 30658560 | tf_op jit(solution)/shard_map/dot_general | solution.py:59
  236.5 13.1 %add_bitcast_fusion.1 = f32[2048,1856]{0,1:T(8,128)} fusion(f32[1856,2048]{1,0:T(8,128)} %fusion.10, bf16[32,1856]{1,0:T(8,128)(2,1)S(1)} %all_gather.22, bf16[1,32,2048]{2,1,0:T(8,128)(2,1)S(1)} %copy.14), kind=kOutput, calls=%fused_computation.1 | convolution fusion | flops 247070720 | bytes 30658560 | tf_op jit(solution)/shard_map/dot_general | solution.py:56
  249.7 43.3 %all-reduce.10 = (bf16[32,2048]{1,0:T(8,128)(2,1)S(1)}, bf16[32,2048]{1,0:T(8,128)(2,1)S(1)}) all-reduce(f32[32,2048]{1,0:T(8,128)S(1)} %convolution_add_fusion.1, f32[32,2048]{1,0:T(8,128)S(1)} %convolution_add_fusion.2), channel_id=7, replica_groups=mesh['seq'=8,'tp'=4] {'seq'}, use_global_device_ids=true, to_apply=%region_7.9.clone | all-reduce | flops 131072 | bytes 786432
  (65 shorter events, 8.7 us)
Async XLA Ops:
  7.2 158.0 %all-reduce.9.cloned.1.call-start = ((), (), s32[]{:S(2)}) async-start(), calls=%async_computation | async-start | bytes 2949120 | tf_op jit(solution)/shard_map/psum | solution.py:34
  7.2 50.3 %copy-start = (bf16[2048,1856]{0,1:T(8,128)(2,1)S(1)}, bf16[2048,1856]{0,1:T(8,128)(2,1)}, u32[]{:S(2)}) copy-start(bf16[2048,1856]{0,1:T(8,128)(2,1)} %param.10) | copy-start | bytes 22806532
  8.1 40.5 %collective-permute-start = (bf16[4,2048]{1,0:T(4,128)(2,1)S(1)}, bf16[4,2048]{1,0:T(4,128)(2,1)S(1)}, u32[]{:S(2)}, u32[]{:S(2)}) collective-permute-start(bf16[4,2048]{1,0:T(4,128)(2,1)S(1)} %get-tuple-element.17), channel_id=1, source_target_pairs={{0,4},{4,8},{8,12},{12,16},{16,20},{20,24},{24,28},{28,0},{1,5},{5... | collective-permute-start | bytes 49160 | tf_op jit(solution)/shard_map/ppermute | solution.py:12
  11.2 6.4 %collective-permute-start.7 = (bf16[4,2048]{1,0:T(4,128)(2,1)S(1)}, bf16[4,2048]{1,0:T(4,128)(2,1)S(1)}, u32[]{:S(2)}, u32[]{:S(2)}) collective-permute-start(bf16[4,2048]{1,0:T(4,128)(2,1)S(1)} %get-tuple-element.18), channel_id=1, source_target_pairs={{0,4},{4,8},{8,12},{12,16},{16,20},{20,24},{24,28},{28,0},{1,5},{5... | collective-permute-start | bytes 49160 | tf_op jit(solution)/shard_map/ppermute | solution.py:12
  17.6 33.1 %collective-permute-start.8 = (bf16[4,2048]{1,0:T(4,128)(2,1)S(1)}, bf16[4,2048]{1,0:T(4,128)(2,1)S(1)}, u32[]{:S(2)}, u32[]{:S(2)}) collective-permute-start(bf16[4,2048]{1,0:T(4,128)(2,1)S(1)} %collective-permute-done.7), channel_id=1, source_target_pairs={{0,4},{4,8},{8,12},{12,16},{16,20},{20,24},{24,28},{28,0},{1,5},{5... | collective-permute-start | bytes 49160 | tf_op jit(solution)/shard_map/ppermute | solution.py:12
  48.6 48.5 %slice-start = ((s8[7602176]{0:T(1024)(128)(4,1)}), s8[4194304]{0:T(1024)(128)(4,1)S(1)}, s32[]{:S(2)}) async-start(s8[7602176]{0:T(1024)(128)(4,1)} %bitcast.50), calls=%async_computation.1 | async-start | bytes 8388608
  48.7 8.3 %collective-permute-start.1 = (bf16[4,2048]{1,0:T(4,128)(2,1)S(1)}, bf16[4,2048]{1,0:T(4,128)(2,1)S(1)}, u32[]{:S(2)}, u32[]{:S(2)}) collective-permute-start(bf16[4,2048]{1,0:T(4,128)(2,1)S(1)} %collective-permute-done), channel_id=1, source_target_pairs={{0,4},{4,8},{8,12},{12,16},{16,20},{20,24},{24,28},{28,0},{1,5},{5... | collective-permute-start | bytes 49160 | tf_op jit(solution)/shard_map/ppermute | solution.py:12
  50.7 6.7 %collective-permute-start.9 = (bf16[4,2048]{1,0:T(4,128)(2,1)S(1)}, bf16[4,2048]{1,0:T(4,128)(2,1)S(1)}, u32[]{:S(2)}, u32[]{:S(2)}) collective-permute-start(bf16[4,2048]{1,0:T(4,128)(2,1)S(1)} %collective-permute-done.8), channel_id=1, source_target_pairs={{0,4},{4,8},{8,12},{12,16},{16,20},{20,24},{24,28},{28,0},{1,5},{5... | collective-permute-start | bytes 49160 | tf_op jit(solution)/shard_map/ppermute | solution.py:12
  56.9 40.2 %slice-start.1 = ((s8[7602176]{0:T(1024)(128)(4,1)}), s8[3407872]{0:T(1024)(128)(4,1)S(1)}, s32[]{:S(2)}) async-start(s8[7602176]{0:T(1024)(128)(4,1)} %bitcast.50), calls=%async_computation.2 | async-start | bytes 6815744
  57.0 6.4 %collective-permute-start.2 = (bf16[4,2048]{1,0:T(4,128)(2,1)S(1)}, bf16[4,2048]{1,0:T(4,128)(2,1)S(1)}, u32[]{:S(2)}, u32[]{:S(2)}) collective-permute-start(bf16[4,2048]{1,0:T(4,128)(2,1)S(1)} %collective-permute-done.1), channel_id=1, source_target_pairs={{0,4},{4,8},{8,12},{12,16},{16,20},{20,24},{24,28},{28,0},{1,5},{5... | collective-permute-start | bytes 49160 | tf_op jit(solution)/shard_map/ppermute | solution.py:12
  57.4 6.7 %collective-permute-start.10 = (bf16[4,2048]{1,0:T(4,128)(2,1)S(1)}, bf16[4,2048]{1,0:T(4,128)(2,1)S(1)}, u32[]{:S(2)}, u32[]{:S(2)}) collective-permute-start(bf16[4,2048]{1,0:T(4,128)(2,1)S(1)} %collective-permute-done.9), channel_id=1, source_target_pairs={{0,4},{4,8},{8,12},{12,16},{16,20},{20,24},{24,28},{28,0},{1,5},{5... | collective-permute-start | bytes 49160 | tf_op jit(solution)/shard_map/ppermute | solution.py:12
  63.4 32.9 %collective-permute-start.3 = (bf16[4,2048]{1,0:T(4,128)(2,1)S(1)}, bf16[4,2048]{1,0:T(4,128)(2,1)S(1)}, u32[]{:S(2)}, u32[]{:S(2)}) collective-permute-start(bf16[4,2048]{1,0:T(4,128)(2,1)S(1)} %collective-permute-done.2), channel_id=1, source_target_pairs={{0,4},{4,8},{8,12},{12,16},{16,20},{20,24},{24,28},{28,0},{1,5},{5... | collective-permute-start | bytes 49160 | tf_op jit(solution)/shard_map/ppermute | solution.py:12
  64.1 33.0 %collective-permute-start.11 = (bf16[4,2048]{1,0:T(4,128)(2,1)S(1)}, bf16[4,2048]{1,0:T(4,128)(2,1)S(1)}, u32[]{:S(2)}, u32[]{:S(2)}) collective-permute-start(bf16[4,2048]{1,0:T(4,128)(2,1)S(1)} %collective-permute-done.10), channel_id=1, source_target_pairs={{0,4},{4,8},{8,12},{12,16},{16,20},{20,24},{24,28},{28,0},{1,5},{5... | collective-permute-start | bytes 49160 | tf_op jit(solution)/shard_map/ppermute | solution.py:12
  96.3 6.5 %collective-permute-start.4 = (bf16[4,2048]{1,0:T(4,128)(2,1)S(1)}, bf16[4,2048]{1,0:T(4,128)(2,1)S(1)}, u32[]{:S(2)}, u32[]{:S(2)}) collective-permute-start(bf16[4,2048]{1,0:T(4,128)(2,1)S(1)} %collective-permute-done.3), channel_id=1, source_target_pairs={{0,4},{4,8},{8,12},{12,16},{16,20},{20,24},{24,28},{28,0},{1,5},{5... | collective-permute-start | bytes 49160 | tf_op jit(solution)/shard_map/ppermute | solution.py:12
  97.1 6.4 %collective-permute-start.12 = (bf16[4,2048]{1,0:T(4,128)(2,1)S(1)}, bf16[4,2048]{1,0:T(4,128)(2,1)S(1)}, u32[]{:S(2)}, u32[]{:S(2)}) collective-permute-start(bf16[4,2048]{1,0:T(4,128)(2,1)S(1)} %collective-permute-done.11), channel_id=1, source_target_pairs={{0,4},{4,8},{8,12},{12,16},{16,20},{20,24},{24,28},{28,0},{1,5},{5... | collective-permute-start | bytes 49160 | tf_op jit(solution)/shard_map/ppermute | solution.py:12
  102.8 6.4 %collective-permute-start.5 = (bf16[4,2048]{1,0:T(4,128)(2,1)S(1)}, bf16[4,2048]{1,0:T(4,128)(2,1)S(1)}, u32[]{:S(2)}, u32[]{:S(2)}) collective-permute-start(bf16[4,2048]{1,0:T(4,128)(2,1)S(1)} %collective-permute-done.4), channel_id=1, source_target_pairs={{0,4},{4,8},{8,12},{12,16},{16,20},{20,24},{24,28},{28,0},{1,5},{5... | collective-permute-start | bytes 49160 | tf_op jit(solution)/shard_map/ppermute | solution.py:12
  103.5 6.4 %collective-permute-start.13 = (bf16[4,2048]{1,0:T(4,128)(2,1)S(1)}, bf16[4,2048]{1,0:T(4,128)(2,1)S(1)}, u32[]{:S(2)}, u32[]{:S(2)}) collective-permute-start(bf16[4,2048]{1,0:T(4,128)(2,1)S(1)} %collective-permute-done.12), channel_id=1, source_target_pairs={{0,4},{4,8},{8,12},{12,16},{16,20},{20,24},{24,28},{28,0},{1,5},{5... | collective-permute-start | bytes 49160 | tf_op jit(solution)/shard_map/ppermute | solution.py:12
  109.2 7.1 %collective-permute-start.6 = (bf16[4,2048]{1,0:T(4,128)(2,1)S(1)}, bf16[4,2048]{1,0:T(4,128)(2,1)S(1)}, u32[]{:S(2)}, u32[]{:S(2)}) collective-permute-start(bf16[4,2048]{1,0:T(4,128)(2,1)S(1)} %collective-permute-done.5), channel_id=1, source_target_pairs={{0,4},{4,8},{8,12},{12,16},{16,20},{20,24},{24,28},{28,0},{1,5},{5... | collective-permute-start | bytes 49160 | tf_op jit(solution)/shard_map/ppermute | solution.py:12
  110.1 12.6 %copy-start.6 = (u32[32]{0:T(128)S(1)}, u32[32]{0:T(128)}, u32[]{:S(2)}) copy-start(u32[32]{0:T(128)} %constant.49) | copy-start | bytes 388
  110.1 13.2 %copy-start.5 = (u32[32]{0:T(128)S(1)}, u32[32]{0:T(128)}, u32[]{:S(2)}) copy-start(u32[32]{0:T(128)} %constant.45) | copy-start | bytes 388
  176.2 7.8 %copy-start.3 = (f32[32,1856]{1,0:T(8,128)S(1)}, f32[32,1856]{1,0:T(8,128)}, u32[]{:S(2)}) copy-start(f32[32,1856]{1,0:T(8,128)} %get-tuple-element.7) | copy-start | bytes 712708
  176.2 7.8 %copy-start.4 = (f32[32,1856]{1,0:T(8,128)S(1)}, f32[32,1856]{1,0:T(8,128)}, u32[]{:S(2)}) copy-start(f32[32,1856]{1,0:T(8,128)} %get-tuple-element.9) | copy-start | bytes 712708
  184.0 27.2 %slice-start.4 = ((s8[7602176]{0:T(1024)(128)(4,1)}), s8[4194304]{0:T(1024)(128)(4,1)S(1)}, s32[]{:S(2)}) async-start(s8[7602176]{0:T(1024)(128)(4,1)} %bitcast.54), calls=%async_computation.5 | async-start | bytes 8388608
  184.0 28.6 %slice-start.2 = ((s8[7602176]{0:T(1024)(128)(4,1)}), s8[3407872]{0:T(1024)(128)(4,1)S(1)}, s32[]{:S(2)}) async-start(s8[7602176]{0:T(1024)(128)(4,1)} %bitcast.52), calls=%async_computation.3 | async-start | bytes 6815744
  186.2 25.0 %slice-start.5 = ((s8[7602176]{0:T(1024)(128)(4,1)}), s8[3407872]{0:T(1024)(128)(4,1)S(1)}, s32[]{:S(2)}) async-start(s8[7602176]{0:T(1024)(128)(4,1)} %bitcast.54), calls=%async_computation.6 | async-start | bytes 6815744
  203.4 9.2 %slice-start.3 = ((s8[7602176]{0:T(1024)(128)(4,1)}), s8[4194304]{0:T(1024)(128)(4,1)S(1)}, s32[]{:S(2)}) async-start(s8[7602176]{0:T(1024)(128)(4,1)} %bitcast.52), calls=%async_computation.4 | async-start | bytes 8388608
  214.1 1.4 copy-start.1
  214.1 1.4 copy-start.2
Sparse Core Ops, SparseCore 0:
  122.8 42.2 all-reduce.8
